TPU v7x, 32 devices: a whole 2x2x4 slice. The times are simulated.
32 devices in a mesh: stn: 8 (over z, core), chan: 4 (over y, x).
Axes of the slice: x: 2, y: 2, z: 4, core: 2. Of those that a mesh axis runs over, the one named last changes fastest.
Arguments:
- voltages: bfloat16 [8, 2, 256, 131072], P('stn', None, None, 'chan'), may hold values from -6 to 6
- positions: float32 [8, 3, 256], P('stn'), may hold values from -4 to 4
- directions: float32 [3, 64], replicated, may hold values from -0.5 to 0.5
- flag_mask: int32 [8, 2, 2048], P('stn', None, 'chan'), may hold values from 0 to 1, as said below
- tapers: float32 [8, 8], P('stn'), may hold values from 0.3 to 3
- weight_index: int32 [8, 64], P('stn'), may hold values from 0 to 7
Outputs:
- beam_power: float32 [64, 131072], P('stn', 'chan')
- beam_total: float32 [64], P('stn')
Inputs may be any that keep to these rules, and one draw needn't show every extreme that they name: `flag_mask`: the first block of station 0 is kept in every channel.
All inputs are finite; a program needn't handle non-finite values.
Results may differ from a plain program's by a relative error of at most 0.003.
Values sent between devices are 32-bit elements; how exact they have to be, the bound alone decides.
A program may use at most 256 MiB of HBM per device.

v0:
```python
import math

import jax
import jax.numpy as jnp
from jax import lax
from jax.sharding import PartitionSpec as P

BLOCK = 128


def station_beam(volts, place, keep_flags, weight_row, directions, ratio):
    delay = (
        directions[0][:, None] * place[0][None, :]
        + directions[1][:, None] * place[1][None, :]
        + directions[2][:, None] * place[2][None, :]
    )
    phase = 2.0 * math.pi * delay[:, :, None] * ratio[None, None, :]
    blocks = keep_flags.shape[0]
    chan_local = keep_flags.shape[1]
    keep = jnp.broadcast_to(
        keep_flags.astype(jnp.float32)[:, None, :], (blocks, BLOCK, chan_local)
    ).reshape(blocks * BLOCK, chan_local)
    amplitude = weight_row[:, None, None] * keep[None, :, :]
    steer_real = (amplitude * jnp.cos(phase)).astype(jnp.bfloat16)
    steer_imag = (-amplitude * jnp.sin(phase)).astype(jnp.bfloat16)
    upper = jnp.concatenate((steer_real, -steer_imag), axis=1)
    lower = jnp.concatenate((steer_imag, steer_real), axis=1)
    steer_block = jnp.concatenate((upper, lower), axis=0)
    signal = volts.reshape(2 * volts.shape[1], chan_local, -1)
    return jnp.einsum("pkc,kct->pct", steer_block, signal, preferred_element_type=jnp.float32)


def on_device(voltages, positions, directions, flag_mask, tapers, weight_index):
    chan_local = flag_mask.shape[2]
    beam_count = directions.shape[1]
    first_channel = lax.axis_index("chan") * chan_local
    chan_whole = chan_local * lax.axis_size("chan")
    ratio = (first_channel + jnp.arange(chan_local)).astype(jnp.float32) / chan_whole
    ratio = 1.0 + 0.5 * ratio
    choose = (weight_index[:, :, None] == jnp.arange(tapers.shape[1])[None, None, :]).astype(
        jnp.float32
    )
    station_weight = jnp.sum(choose * tapers[:, None, :], axis=2)
    alive = jnp.sum(flag_mask, axis=1).astype(jnp.float32) * BLOCK
    counts = jnp.dot(station_weight.T, alive, precision=lax.Precision.HIGHEST)
    partial_value = station_beam(
        voltages[0], positions[0], flag_mask[0], station_weight[0], directions, ratio
    )
    partial_value = partial_value.reshape(2, beam_count, -1).transpose(1, 0, 2)
    rows = beam_count // lax.axis_size("stn")
    mine, counts_mine = (
        lax.psum_scatter(partial_value, "stn", scatter_dimension=0, tiled=True),
        lax.psum_scatter(counts, "stn", scatter_dimension=0, tiled=True),
    )
    scaled = mine.reshape(rows, 2, chan_local, -1) / counts_mine[:, None, :, None]
    power = scaled[:, 0] * scaled[:, 0] + scaled[:, 1] * scaled[:, 1]
    beam_power = power.reshape(rows, -1)
    beam_total = lax.psum(jnp.sum(beam_power, axis=1), "chan")
    return (beam_power, beam_total)


def solution(mesh):
    in_specs = (
        P("stn", None, None, "chan"),
        P("stn", None, None),
        P(),
        P("stn", None, "chan"),
        P("stn", None),
        P("stn", None),
    )
    out_specs = (P("stn", "chan"), P("stn"))
    return jax.shard_map(
        on_device, mesh=mesh, in_specs=in_specs, out_specs=out_specs, check_vma=False
    )
```

profile of v0, /device:TPU:0, one launch (start us, length us, event | category | flops | bytes accessed | tf_op | source)
XLA Modules:
  0.0 725.6 jit_solution(12028683576861649226)
XLA Ops:
  7.2 0.0 reduce-scatter.3.cloned.1.call-start
  7.2 0.7 fusion.20
  7.9 0.8 slice_bitcast_fusion.2
  8.7 1.4 fusion.19
  10.1 0.1 copy.17
  10.2 0.6 broadcast_in_dim.2
  10.9 0.8 select_reduce_fusion
  11.7 0.1 add_multiply_fusion
  11.8 126.0 %fusion.10 = (bf16[64,256,512]{1,0,2:T(8,128)(2,1)}, bf16[64,256,512]{1,0,2:T(8,128)(2,1)}) fusion(f32[512]{0:T(512)S(1)} %multiply_add_fusion, f32[64,256]{1,0:T(8,128)S(1)} %add_multiply_fusion, f32[256,512]{0,1:T(8,128)S(1)} %bitcast.36, f32[64]{0:T(128)S(1)} %select_reduce_fusion), kind=kLoop, calls=%fused_computation.14 | loop fusion | flops 58720256 | bytes 34146560 | tf_op jit(solution)/shard_map/convert_element_type | solution.py:25
  137.7 116.4 %fusion.16 = bf16[64,256,512]{1,0,2:T(8,128)(2,1)} fusion(f32[512]{0:T(512)S(1)} %multiply_add_fusion, f32[64,256]{1,0:T(8,128)S(1)} %add_multiply_fusion, f32[256,512]{0,1:T(8,128)S(1)} %bitcast.37, f32[64]{0:T(128)S(1)} %select_reduce_fusion), kind=kLoop, calls=%fused_computation.32 | loop fusion | flops 67108864 | bytes 17369344 | tf_op jit(solution)/shard_map/neg | solution.py:26
  254.1 80.2 %copy.18 = bf16[1,2,256,32768]{2,1,3,0:T(2,128)(2,1)} copy(bf16[1,2,256,32768]{3,2,1,0:T(8,128)(2,1)} %param.6) | data formatting | bytes 67108864 | tf_op args[0]
  334.4 52.7 %reshape_squeeze.3 = bf16[512,512,64]{0,2,1:T(8,128)(2,1)} reshape(bf16[1,2,256,32768]{2,1,3,0:T(2,128)(2,1)} %copy.18) | data formatting | bytes 67108864 | tf_op jit(solution)/shard_map/reshape;squeeze | solution.py:29
  387.1 41.6 %fusion.11 = f32[128,512,64]{0,2,1:T(8,128)} fusion(bf16[512,512,64]{0,2,1:T(8,128)(2,1)} %reshape_squeeze.3, bf16[64,256,512]{1,0,2:T(8,128)(2,1)} %get-tuple-element.5, bf16[64,256,512]{1,0,2:T(8,128)(2,1)} %get-tuple-element.4, bf16[64,256,512]{1,0,2:T(8,128)(2,1)} %fusion.16), kind=kOutput, calls=%fused_computation.15 | convolution fusion | flops 4563402752 | bytes 100663296 | tf_op jit(solution)/shard_map/pkc,kct->pct/dot_general | solution.py:30
  428.7 32.3 %reshape.225 = f32[2,64,32768]{1,0,2:T(2,128)} reshape(f32[128,512,64]{0,2,1:T(8,128)} %fusion.11) | data formatting | bytes 33554432 | tf_op jit(solution)/shard_map/reshape | solution.py:49
  461.1 39.6 %copy.20 = f32[2,64,32768]{2,1,0:T(8,128)} copy(f32[2,64,32768]{1,0,2:T(2,128)} %reshape.225) | data formatting | bytes 33554432 | tf_op jit(solution)/shard_map/reshape | solution.py:49
  500.7 0.0 reduce-scatter.5.cloned.1.call-start
  500.7 0.7 broadcast_multiply_fusion
  501.5 170.2 %reduce-scatter.3.cloned.1.call-done = f32[8,2,32768]{2,0,1:T(8,128)} async-done(((f32[64,2,32768]{2,0,1:T(8,128)}), f32[8,2,32768]{2,0,1:T(8,128)}) %reduce-scatter.3.cloned.1.call-update) | async-done | bytes 2097168 | tf_op jit(solution)/shard_map/reduce_scatter | solution.py:52
  671.7 4.2 reshape.224
  675.9 27.7 %reduce-scatter.5.cloned.1.call-done = f32[8,512]{1,0:T(8,128)} async-done(((f32[64,512]{1,0:T(8,128)}), f32[8,512]{1,0:T(8,128)}) %reduce-scatter.5.cloned.1.call-update) | async-done | bytes 16400 | tf_op jit(solution)/shard_map/reduce_scatter | solution.py:53
  703.6 2.7 broadcast_divide_fusion
  706.3 0.5 fusion.17
  706.8 1.6 add.55
  708.5 10.3 %psum.7 = f32[8]{0:T(128)} all-reduce(f32[8]{0:T(128)S(1)} %get-tuple-element.2), channel_id=1, replica_groups=mesh['stn'=8,'chan'=4] {'chan'}, use_global_device_ids=true, to_apply=%region_5.0 | all-reduce | flops 8 | bytes 64 | tf_op jit(solution)/shard_map/psum | solution.py:58
  (11 shorter events, 0.1 us)
Async XLA Ops:
  7.2 664.5 %reduce-scatter.3.cloned.1.call-start = ((), (), s32[]{:S(2)}) async-start(), calls=%async_computation.2 | async-start | bytes 18874368 | tf_op jit(solution)/shard_map/reduce_scatter | solution.py:52
  11.7 126.1 %copy-start.1 = (f32[64]{0:T(128)}, f32[64]{0:T(128)S(1)}, u32[]{:S(2)}) copy-start(f32[64]{0:T(128)S(1)} %select_reduce_fusion) | copy-start | bytes 772
  461.0 39.7 %copy-start = (s32[512]{0:T(512)S(1)}, s32[512]{0:T(512)}, u32[]{:S(2)}) copy-start(s32[512]{0:T(512)} %get-tuple-element.6) | copy-start | bytes 6148
  461.0 39.7 %copy-start.2 = (f32[64]{0:T(128)S(1)}, f32[64]{0:T(128)}, u32[]{:S(2)}) copy-start(f32[64]{0:T(128)} %copy-done.1) | copy-start | bytes 772
  500.7 202.9 %reduce-scatter.5.cloned.1.call-start = ((), (), s32[]{:S(2)}) async-start(), calls=%async_computation.3 | async-start | bytes 147456 | tf_op jit(solution)/shard_map/reduce_scatter | solution.py:53
Sparse Core Ops, SparseCore 0:
  500.8 170.8 reduce-scatter.2
  674.5 29.0 reduce-scatter.4
where the time goes:
time: 731 us; the launch traced here: 726 us
  other arithmetic  249 us (34%)
  local copies, waits for them, and re-layouts  213 us (29%)
  waiting for transfers between devices  198 us (27%)
  matrix products  41.6 us (6%)
  between operations  14.1 us (2%)
  blocking collectives  10.3 us (1%)
    reduce_scatter x1, waiting for transfers between devices, on_device(): lax.psum_scatter(partial_value, 'stn', scatter_dimension=0, tiled=True)  170 us
    convert_element_type x1, other arithmetic, station_beam(): steer_imag = (-amplitude * jnp.sin(phase)).astype(jnp.bfloat16)  126 us
    neg x1, other arithmetic, station_beam(): upper = jnp.concatenate((steer_real, -steer_imag), axis=1)  116 us
    unnamed x8, local copies, waits for them, and re-layouts  80.3 us
    reshape x2, local copies, waits for them, and re-layouts, on_device(): partial_value = partial_value.reshape(2, beam_count, -1).transpose(1, 0, 2)  71.9 us
    another operation x1, local copies, waits for them, and re-layouts, station_beam(): signal = volts.reshape(2 * volts.shape[1], chan_local, -1)  52.7 us
    dot_general x1, matrix products, station_beam(): jnp.einsum('pkc,kct->pct', steer_block, signal, preferred_element_type=jn...  41.6 us
    reduce_scatter x1, waiting for transfers between devices, on_device(): lax.psum_scatter(counts, 'stn', scatter_dimension=0, tiled=True)  27.7 us
  transfers between devices with their start and end apart: 2, of which 2 were waited for; matrix products, arithmetic and copies ran while one was open for 1% of the time, Pallas kernels for 0%

commit v1 on v0

v1 whole, which is shorter than its diff:
```python
import functools
import math

import jax
import jax.numpy as jnp
from jax import lax
from jax.experimental import pallas as pl
from jax.experimental.pallas import tpu as pltpu
from jax.sharding import PartitionSpec as P

BLOCK = 128
LANES = 128
STEP = 8
MESH = pl.DeviceIdType.MESH


def turn(u):
    quarter = jnp.floor(u * 4.0 + 0.5)
    x = (u - quarter * 0.25) * (2.0 * math.pi)
    x2 = x * x
    s = x * (1.0 + x2 * (-1.0 / 6 + x2 * (1.0 / 120 + x2 * (-1.0 / 5040 + x2 * (1.0 / 362880)))))
    c = 1.0 + x2 * (-0.5 + x2 * (1.0 / 24 + x2 * (-1.0 / 720 + x2 * (1.0 / 40320))))
    q = quarter - 4.0 * jnp.floor(quarter * 0.25)
    odd = (q == 1.0) | (q == 3.0)
    cos = jnp.where(odd, s, c)
    sin = jnp.where(odd, c, s)
    cos = jnp.where((q == 1.0) | (q == 2.0), -cos, cos)
    sin = jnp.where(q >= 2.0, -sin, sin)
    return cos, sin


def kernel(
    dims, gap, volts, flags, delay, weight, counts_part, power, total,
    vbuf, part, peer, hop, base, fine, counts_in, counts_all, sums,
    v_sem, x_send, x_recv, h_send, h_recv, c_send, c_recv, t_send, t_recv,
):
    n, nchan, chips, rows, chan_local, samples, group, chunks, half = dims
    me = lax.axis_index("stn")
    col = lax.axis_index("chan")
    chip, core = lax.div(me, 2), lax.rem(me, 2)
    lanes = 2 * half

    def fetch(i):
        return pltpu.make_async_copy(
            volts.at[:, :, pl.ds(pl.multiple_of(i * lanes, lanes), lanes)],
            vbuf.at[lax.rem(i, 3)],
            v_sem.at[lax.rem(i, 3)],
        )

    for i in range(min(2, chunks)):
        fetch(i).start()

    barrier = pltpu.get_barrier_semaphore()
    for r in range(1, n):
        pl.semaphore_signal(barrier, 1, device_id=(lax.rem(me + r, n), col), device_id_type=MESH)
    for r in range(1, nchan):
        pl.semaphore_signal(barrier, 1, device_id=(me, lax.rem(col + r, nchan)), device_id_type=MESH)

    chan_whole = chan_local * nchan
    for i in range(STEP):
        c, s = turn(delay[...] * (0.5 * i / chan_whole))
        fine[i, 0] = c
        fine[i, 1] = -s
    sums[pl.ds(col, 1)] = jnp.zeros((1, rows, LANES), jnp.float32)

    pl.semaphore_wait(barrier, n - 1 + nchan - 1)

    def counts_copy(r):
        to = lax.rem(me + r, n)
        return pltpu.make_async_remote_copy(
            src_ref=counts_part.at[to], dst_ref=counts_in.at[r - 1],
            send_sem=c_send.at[r - 1], recv_sem=c_recv.at[r - 1],
            device_id=(to, col), device_id_type=MESH,
        )

    for r in range(1, n):
        counts_copy(r).start()

    def peer_copy(i):
        return pltpu.make_async_remote_copy(
            src_ref=part.at[i, 1 - core], dst_ref=peer.at[i],
            send_sem=x_send.at[i], recv_sem=x_recv.at[i],
            device_id=(chip * 2 + 1 - core, col), device_id_type=MESH,
        )

    def hop_copy(i, way, k):
        to = lax.rem(chip + (1 if way == 0 else chips - 1), chips) * 2 + core
        if k == 0:
            block = lax.rem(chip + (chips - 1 if way == 0 else 1), chips)
            src = peer.at[i, way, block]
        else:
            src = hop.at[way, k - 1, i]
        return pltpu.make_async_remote_copy(
            src_ref=src, dst_ref=hop.at[way, k, i],
            send_sem=h_send.at[way, k, i], recv_sem=h_recv.at[way, k, i],
            device_id=(to, col), device_id_type=MESH,
        )

    pair_lane = lax.broadcasted_iota(jnp.int32, (1, LANES), 1)
    first_half = pair_lane < samples

    def compute(i):
        slot = lax.rem(i, 3)
        fetch(i).wait()

        @pl.when(i + 2 < chunks)
        def _():
            fetch(i + 2).start()

        steps = group // STEP

        def one(j, carry):
            channel = i * group + j * STEP
            ratio = 1.0 + (0.5 / chan_whole) * (col * chan_local + channel).astype(jnp.float32)
            c, s = turn(delay[...] * ratio)
            base[0] = weight[...] * c
            base[1] = -weight[...] * s
            way = lax.div(j, steps // 2)
            inner = lax.rem(j, steps // 2)
            for p in range(STEP // 2):
                tiles = []
                for q in range(2):
                    real, imag = [], []
                    for k in range(fine.shape[3] // BLOCK):
                        cut = slice(k * BLOCK, (k + 1) * BLOCK)
                        keep = flags[k, channel + 2 * p + q].astype(jnp.float32)
                        br = fine[2 * p + q, 0, :, cut]
                        bi = fine[2 * p + q, 1, :, cut]
                        ar = base[0, :, cut] * keep
                        ai = base[1, :, cut] * keep
                        real.append((ar * br - ai * bi).astype(jnp.bfloat16))
                        imag.append((ar * bi + ai * br).astype(jnp.bfloat16))
                    tiles += [jnp.concatenate(real, axis=1), jnp.concatenate(imag, axis=1)]
                steer = jnp.concatenate(tiles, axis=0)
                at = pl.ds(pl.multiple_of(j * STEP * samples + p * LANES, LANES), LANES)
                signal = jnp.concatenate([vbuf[slot, 0, :, at], vbuf[slot, 1, :, at]], axis=1)
                out = jnp.dot(steer, signal, preferred_element_type=jnp.float32)
                beams = out.shape[0] // 4
                rr = [out[g * beams:(g + 1) * beams, :LANES] for g in range(4)]
                ri = [out[g * beams:(g + 1) * beams, LANES:] for g in range(4)]
                re = jnp.where(first_half, rr[0], rr[2]) - jnp.where(first_half, ri[1], ri[3])
                im = jnp.where(first_half, rr[1], rr[3]) + jnp.where(first_half, ri[0], ri[2])
                to = pl.ds(pl.multiple_of(inner * STEP * samples + p * LANES, LANES), LANES)
                for d in range(n):
                    own = slice(d * rows, (d + 1) * rows)
                    part[i, d % 2, way, d // 2, 0:rows, to] = re[own]
                    part[i, d % 2, way, d // 2, rows:2 * rows, to] = im[own]
            return carry

        lax.fori_loop(0, steps, one, 0)
        peer_copy(i).start()

    def pair_sum(i):
        peer_copy(i).wait_recv()
        for way in range(2):
            for d in range(chips):
                peer[i, way, d] = peer[i, way, d] + part[i, core, way, d]
        for way in range(2):
            hop_copy(i, way, 0).start()

    def forward(i, k):
        for way in range(2):
            hop_copy(i, way, k).wait_recv()
            block = lax.rem(chip + ((2 * chips - 2 - k) if way == 0 else (2 + k)), chips)
            hop[way, k, i] = hop[way, k, i] + peer[i, way, block]
            hop_copy(i, way, k + 1).start()

    def finish(i):
        per = LANES // group
        tile = counts_all[lax.div(i, per)]
        tile = pltpu.roll(tile, lax.rem(LANES - lax.rem(i, per) * group, LANES), 1)
        inverse = 1.0 / tile
        for way in range(2):
            k = chips - 2
            hop_copy(i, way, k).wait_recv()
            acc = jnp.zeros((rows, LANES), jnp.float32)
            for b in range(half // LANES):
                cut = slice(b * LANES, (b + 1) * LANES)
                v = hop[way, k, i, :, cut] + peer[i, way, chip, :, cut]
                c0 = way * (group // 2) + 2 * b
                scale = jnp.where(first_half, inverse[:rows, c0:c0 + 1], inverse[:rows, c0 + 1:c0 + 2])
                x = v[:rows] * scale
                y = v[rows:] * scale
                z = x * x + y * y
                power[:, pl.ds(pl.multiple_of(i * lanes + way * half + b * LANES, LANES), LANES)] = z
                acc = acc + z
            sums[pl.ds(col, 1)] = sums[pl.ds(col, 1)] + acc[None]

    last = 1 + gap * (chips - 1)

    def iteration(it, carry):
        done = it - last

        @pl.when(it == last)
        def _():
            acc = counts_part[me]
            for r in range(1, n):
                counts_copy(r).wait_recv()
                acc = acc + counts_in[r - 1]
            counts_all[...] = acc

        @pl.when(done >= 0)
        def _():
            finish(done)

        for k in range(chips - 3, -1, -1):
            at = it - 1 - gap * (k + 1)

            @pl.when((at >= 0) & (at < chunks))
            def _():
                forward(at, k)

        @pl.when((it >= 1) & (it - 1 < chunks))
        def _():
            pair_sum(it - 1)

        @pl.when(it < chunks)
        def _():
            compute(it)

        return carry

    lax.fori_loop(0, chunks + last, iteration, 0)

    def total_copy(r):
        return pltpu.make_async_remote_copy(
            src_ref=sums.at[col], dst_ref=sums.at[col],
            send_sem=t_send.at[r - 1], recv_sem=t_recv.at[r - 1],
            device_id=(me, lax.rem(col + r, nchan)), device_id_type=MESH,
        )

    def total_wait(r):
        src = lax.rem(col + nchan - r, nchan)
        pltpu.make_async_remote_copy(
            src_ref=sums.at[src], dst_ref=sums.at[src],
            send_sem=t_send.at[r - 1], recv_sem=t_recv.at[r - 1],
            device_id=(me, src), device_id_type=MESH,
        ).wait_recv()

    for r in range(1, nchan):
        total_copy(r).start()

    def drain(i, carry):
        peer_copy(i).wait_send()
        for way in range(2):
            for k in range(chips - 1):
                hop_copy(i, way, k).wait_send()
        return carry

    lax.fori_loop(0, chunks, drain, 0)
    for r in range(1, n):
        counts_copy(r).wait_send()
    for r in range(1, nchan):
        total_wait(r)
    acc = sums[0]
    for r in range(1, nchan):
        acc = acc + sums[r]
    total[...] = jnp.broadcast_to(jnp.sum(acc, axis=1, keepdims=True), (rows, LANES))
    for r in range(1, nchan):
        total_copy(r).wait_send()


def on_device(voltages, positions, directions, flag_mask, tapers, weight_index, group=32, gap=2):
    n, nchan = lax.axis_size("stn"), lax.axis_size("chan")
    blocks, chan_local = flag_mask.shape[1:]
    beams = directions.shape[1]
    dipoles = voltages.shape[2]
    samples = voltages.shape[3] // chan_local
    rows, chips = beams // n, n // 2
    chunks = chan_local // group
    half = group // 2 * samples
    place = positions[0]
    delay = (
        directions[0][:, None] * place[0][None, :]
        + directions[1][:, None] * place[1][None, :]
        + directions[2][:, None] * place[2][None, :]
    )
    choose = (weight_index[0][:, None] == jnp.arange(tapers.shape[1])[None, :]).astype(jnp.float32)
    weight = jnp.sum(choose * tapers[0][None, :], axis=1)
    alive = jnp.sum(flag_mask[0], axis=0).astype(jnp.float32) * BLOCK
    counts = (
        weight.reshape(n, 1, rows, 1) * alive.reshape(1, chan_local // LANES, 1, LANES)
    )
    crows = max(rows, 8)
    counts = jnp.concatenate(
        [counts, jnp.ones((n, chan_local // LANES, crows - rows, LANES), jnp.float32)], axis=2
    ) if crows > rows else counts
    dims = (n, nchan, chips, rows, chan_local, samples, group, chunks, half)
    f32 = jnp.float32
    vmem = pl.BlockSpec(memory_space=pltpu.VMEM)
    dma = pltpu.SemaphoreType.DMA
    power, total = pl.pallas_call(
        functools.partial(kernel, dims, gap),
        out_shape=(
            jax.ShapeDtypeStruct((rows, chan_local * samples), f32),
            jax.ShapeDtypeStruct((rows, LANES), f32),
        ),
        in_specs=[
            pl.BlockSpec(memory_space=pl.ANY),
            pl.BlockSpec(memory_space=pltpu.SMEM),
            vmem, vmem, vmem,
        ],
        out_specs=(vmem, vmem),
        scratch_shapes=[
            pltpu.VMEM((3, 2, dipoles, 2 * half), jnp.bfloat16),
            pltpu.VMEM((chunks, 2, 2, chips, 2 * rows, half), f32),
            pltpu.VMEM((chunks, 2, chips, 2 * rows, half), f32),
            pltpu.VMEM((2, chips - 1, chunks, 2 * rows, half), f32),
            pltpu.VMEM((2, beams, dipoles), f32),
            pltpu.VMEM((STEP, 2, beams, dipoles), f32),
            pltpu.VMEM((n - 1, chan_local // LANES, crows, LANES), f32),
            pltpu.VMEM((chan_local // LANES, crows, LANES), f32),
            pltpu.VMEM((nchan, rows, LANES), f32),
            dma((3,)),
            dma((chunks,)),
            dma((chunks,)),
            dma((2, chips - 1, chunks)),
            dma((2, chips - 1, chunks)),
            dma((n - 1,)),
            dma((n - 1,)),
            dma((nchan - 1,)),
            dma((nchan - 1,)),
        ],
        compiler_params=pltpu.CompilerParams(
            collective_id=0, has_side_effects=True, vmem_limit_bytes=60 * 1024 * 1024
        ),
    )(voltages[0], flag_mask[0], delay, jnp.broadcast_to(weight[:, None], delay.shape), counts)
    return power, total[:, 0]


def solution(mesh):
    in_specs = (
        P("stn", None, None, "chan"),
        P("stn", None, None),
        P(),
        P("stn", None, "chan"),
        P("stn", None),
        P("stn", None),
    )
    out_specs = (P("stn", "chan"), P("stn"))
    return jax.shard_map(
        on_device, mesh=mesh, in_specs=in_specs, out_specs=out_specs, check_vma=False
    )
```

time: 731 us -> 164 us (0.22)
  other arithmetic: 249 us -> 2.91 us
  local copies, waits for them, and re-layouts: 213 us -> 5.84 us
  waiting for transfers between devices: 198 us -> 0 us
  Pallas kernels: 0 us -> 155 us
  matrix products: 41.6 us -> 0 us
  between operations: 14.1 us -> 0.64 us
  blocking collectives: 10.3 us -> 0 us
    reduce_scatter x2 -> x0, waiting for transfers between devices: 198 us -> none  [the longest x1 170 us: on_device(): lax.psum_scatter(partial_value, 'stn', scatter_dimension=0, tiled=True)]
    pallas_call x0 -> x1, Pallas kernels: none -> 155 us  [on_device(): pl.pallas_call(functools.partial(kernel, dims, gap), out_shape=(jax.Shape...]
    convert_element_type x1 -> x0, other arithmetic: 126 us -> none  [station_beam(): steer_imag = (-amplitude * jnp.sin(phase)).astype(jnp.bfloat16)]
    neg x1 -> x0, other arithmetic: 116 us -> none  [station_beam(): upper = jnp.concatenate((steer_real, -steer_imag), axis=1)]
    unnamed x8 -> x1, local copies, waits for them, and re-layouts: 80.3 us -> 2.26 us
    reshape x3 -> x0, local copies, waits for them, and re-layouts: 76.1 us -> none  [the longest x2 71.9 us: on_device(): partial_value = partial_value.reshape(2, beam_count, -1).transpose(1, 0, 2)]
    another operation x1 -> x0, local copies, waits for them, and re-layouts: 52.7 us -> none  [station_beam(): signal = volts.reshape(2 * volts.shape[1], chan_local, -1)]
    dot_general x1 -> x0, matrix products: 41.6 us -> none  [station_beam(): jnp.einsum('pkc,kct->pct', steer_block, signal, preferred_element_type=jn...]
  transfers between devices with their start and end apart: 2 -> 0, of which waited for: 2 -> 0; matrix products, arithmetic and copies ran while one was open for 1% -> 0% of each run, Pallas kernels for 0% -> 0%
where the time goes in v1:
time: 164 us
  Pallas kernels  155 us (95%)
  local copies, waits for them, and re-layouts  5.84 us (4%)
  other arithmetic  2.91 us (2%)
    pallas_call x1, Pallas kernels, on_device(): pl.pallas_call(functools.partial(kernel, dims, gap), out_shape=(jax.Shape...  155 us

profile of v1, /device:TPU:0, one launch (start us, length us, event | category | flops | bytes accessed | tf_op | source)
XLA Modules:
  0.0 164.1 jit_solution(5094279676899047657)
XLA Ops:
  0.6 0.8 select_reduce_fusion
  1.4 0.8 slice_bitcast_fusion.2
  2.2 0.7 reduce_sum.19
  2.9 0.7 fusion
  3.6 0.1 mul.107
  3.7 0.7 multiply_add_fusion.delay
  4.4 0.7 broadcast_in_dim.2.weight
  5.1 0.7 broadcast_multiply_fusion.counts_part
  5.8 154.7 %shard_map.77 = (f32[8,32768]{1,0:T(8,128)}, f32[8,128]{1,0:T(8,128)}) custom-call(bf16[2,256,32768]{2,1,0:T(8,128)(2,1)} %bitcast.15, s32[2,512]{1,0:T(2,128)} %bitcast.16, f32[64,256]{1,0:T(8,128)} %multiply_add_fusion.delay, f32[64,256]{1,0:T(8,128)} %broadcast_in_dim.2.weight, f32[8,4,8,128]{3,2,1,0:T(8,128)} %broadcast_multiply_fusion.counts_part), custom_call_target="tpu_custom_call" | custom-call | tf_op jit(solution)/shard_map/pallas_call | solution.py:292
  160.5 1.3 slice_reduce_fusion
  161.8 2.3 %copy.9 = f32[8,32768]{1,0:T(8,128)} copy(f32[8,32768]{1,0:T(8,128)} %get-tuple-element.14) | data formatting | bytes 2097152
  (1 shorter events, 0.0 us)

commit v2 on v1

--- a/solution.py
+++ b/solution.py
@@ -260,7 +260,7 @@
         total_copy(r).wait_send()
 
 
-def on_device(voltages, positions, directions, flag_mask, tapers, weight_index, group=32, gap=2):
+def on_device(voltages, positions, directions, flag_mask, tapers, weight_index, group=16, gap=4):
     n, nchan = lax.axis_size("stn"), lax.axis_size("chan")
     blocks, chan_local = flag_mask.shape[1:]
     beams = directions.shape[1]

time: 164 us -> 167 us (1.018)
  Pallas kernels: 155 us -> 157 us
    pallas_call x1, Pallas kernels: 155 us -> 157 us  [on_device(): pl.pallas_call(functools.partial(kernel, dims, gap), out_shape=(jax.Shape...]
where the time goes in v2:
time: 167 us; the launch traced here: 166 us
  Pallas kernels  157 us (94%)
  local copies, waits for them, and re-layouts  5.84 us (3%)
  other arithmetic  2.91 us (2%)
    pallas_call x1, Pallas kernels, on_device(): pl.pallas_call(functools.partial(kernel, dims, gap), out_shape=(jax.Shape...  157 us

profile of v2, /device:TPU:0, one launch (start us, length us, event | category | flops | bytes accessed | tf_op | source)
XLA Modules:
  0.0 166.5 jit_solution(16892721179108815218)
XLA Ops:
  0.6 0.8 select_reduce_fusion
  1.4 0.8 slice_bitcast_fusion.2
  2.2 0.7 reduce_sum.19
  2.9 0.7 fusion
  3.6 0.1 mul.107
  3.7 0.7 multiply_add_fusion.delay
  4.4 0.7 broadcast_in_dim.2.weight
  5.1 0.7 broadcast_multiply_fusion.counts_part
  5.8 157.1 %shard_map.77 = (f32[8,32768]{1,0:T(8,128)}, f32[8,128]{1,0:T(8,128)}) custom-call(bf16[2,256,32768]{2,1,0:T(8,128)(2,1)} %bitcast.15, s32[2,512]{1,0:T(2,128)} %bitcast.16, f32[64,256]{1,0:T(8,128)} %multiply_add_fusion.delay, f32[64,256]{1,0:T(8,128)} %broadcast_in_dim.2.weight, f32[8,4,8,128]{3,2,1,0:T(8,128)} %broadcast_multiply_fusion.counts_part), custom_call_target="tpu_custom_call" | custom-call | tf_op jit(solution)/shard_map/pallas_call | solution.py:292
  162.9 1.3 slice_reduce_fusion
  164.2 2.3 %copy.9 = f32[8,32768]{1,0:T(8,128)} copy(f32[8,32768]{1,0:T(8,128)} %get-tuple-element.14) | data formatting | bytes 2097152
  (1 shorter events, 0.0 us)
